TPU v7x, 512 devices: a whole 4x8x8 slice. The times are simulated.
512 devices in a mesh: grp: 8 (over y), blk: 64 (over z, x, core).
Axes of the slice: x: 4, y: 8, z: 8, core: 2. Of those that a mesh axis runs over, the one named last changes fastest.
Arguments:
- query_rows: bfloat16 [12288, 4096], P('blk', 'grp'), may hold values from -128 to 128
- key_rows: bfloat16 [12288, 512], P(('grp', 'blk')), may hold values from -6 to 6
- value_rows: bfloat16 [12288, 512], P(('grp', 'blk')), may hold values from -6 to 6
- span_ids: int32 [128], P('blk'), may hold values from 0 to 127, as said below
Outputs:
- attended: bfloat16 [12288, 4096], P('blk', 'grp')
Inputs may be any that keep to these rules, and one draw needn't show every extreme that they name: `span_ids`: A permutation of 0 to 127; each device of blk holds two entries, in device order.
All inputs are finite; a program needn't handle non-finite values.
Results may differ from a plain program's by a relative error of at most 0.0045.
Values may be sent and summed in bfloat16 or wider, within the bound.
No kernel may reach another device: no remote copies, remote signals or barrier semaphores. Data moves between devices by JAX's collectives and lax.ppermute only.
A program may use at most 64 MiB of HBM per device.

v0:
```python
import functools
import math

import jax
import jax.numpy as jnp
from jax import lax
from jax.experimental import pallas as pl
from jax.experimental.pallas import tpu as pltpu
from jax.sharding import Mesh
from jax.sharding import PartitionSpec as P


HEAD_DIM = 128
SPAN = 96
PIECE = 24
ROWS = 784
KEYS = 384
HEADS = 4
COLS = 2 * HEADS * SPAN
STATE = 144
PART = 256
GROUP = 4
MASKED = -1e30
FACTOR = HEAD_DIM**-0.5 * math.log2(math.e)
AXES = ("kv", "pair", "z", "x", "core")
BLK = ("z", "x", "core")
F32 = jnp.float32
BF16 = jnp.bfloat16


def pack_kernel(key_ref, value_ref, ids_ref, out_ref):
    own = jnp.concatenate([ids_ref[...]] * 4, axis=0).astype(BF16)
    for head in range(4):
        lanes = slice(head * HEAD_DIM, (head + 1) * HEAD_DIM)
        for x in range(4):
            out_ref[head, x, 0:24, :] = key_ref[:, lanes]
            out_ref[head, x, 24:48, :] = value_ref[:, lanes]
            out_ref[head, x, 48:56, :] = own


def spread_kernel(routed_ref, out_ref):
    for k in range(4):
        for x in range(4):
            at = (k * 4 + x) * PIECE
            out_ref[0, at : at + PIECE, :] = routed_ref[k, x, 0:24, :]
            out_ref[0, KEYS + at : KEYS + at + PIECE, :] = routed_ref[k, x, 24:48, :]
    rows = []
    for k in range(4):
        ids = sum(routed_ref[k, x, 48:56, :].astype(F32) for x in range(4))
        rows += [ids[0:1], ids[0:1], ids[1:2], ids[1:2]]
    out_ref[0, 2 * KEYS : ROWS, :] = jnp.concatenate(rows, axis=0).astype(BF16)


def reorder(source, out_ref, first):
    for e in range(2):
        for h in range(HEADS):
            at = first + h * SPAN
            out_ref[e, at : at + SPAN, :] = source[
                e * SPAN : (e + 1) * SPAN, h * HEAD_DIM : (h + 1) * HEAD_DIM
            ]


def reorder_kernel(source_ref, out_ref):
    reorder(source_ref, out_ref, 0)


def stack_kernel(own_ref, beyond_ref, ids_ref, out_ref):
    ids = jnp.concatenate([ids_ref[...]] * 8, axis=0).astype(BF16)
    reorder(beyond_ref, out_ref, COLS // 2)
    for e in range(2):
        out_ref[e, 0 : COLS // 2, :] = own_ref[e]
        out_ref[e, COLS : COLS + 16, :] = ids


def attend_kernel(mine, sets, start, width, has_state, last, *refs):
    refs = list(refs)
    q_refs = [refs.pop(0) for _ in sets]
    count = len(mine)
    block = [refs.pop(0) for _ in mine]
    state_ref = refs.pop(0) if has_state else None
    out_ref, turned, masks, one_hot, *held = refs
    weights, held = held[2:], held[:2]
    keys = KEYS * count

    turned[128:144, :] = jnp.ones((16, keys), BF16)
    for b in range(count):
        turned[0:128, b * KEYS : (b + 1) * KEYS] = block[b][0, KEYS : 2 * KEYS, :].T
    spot = lax.broadcasted_iota(jnp.int32, (SPAN, HEAD_DIM), 0)
    mark = lax.broadcasted_iota(jnp.int32, (SPAN, HEAD_DIM), 1)
    spike = jnp.where(spot == mark, 1.0, 0.0).astype(BF16)
    for k in range(2 * HEADS):
        one_hot[k * SPAN : (k + 1) * SPAN, :] = spike

    lane = lax.broadcasted_iota(jnp.int32, (PIECE, HEAD_DIM), 1)
    row = lax.broadcasted_iota(jnp.int32, (PIECE, HEAD_DIM), 0)
    ahead = (row - lane).astype(F32)
    core = lax.axis_index("core")

    def mask(s):
        query_row = q_refs[s // 2][s % 2, COLS : COLS + 16, :].astype(F32)[s % 2 : s % 2 + 1]
        for b in range(count):
            begin = ahead + ((core if mine[b] else 1 - core) * PIECE).astype(F32)
            places = block[b][0, 2 * KEYS : ROWS, :].astype(F32)
            limits = (query_row - places) * float(SPAN)
            for i in range(0, 16, 2):
                pieces = [
                    jnp.where(
                        begin + float(j % 2 * 2 * PIECE)
                        > jnp.broadcast_to(limits[j : j + 1], ahead.shape),
                        MASKED,
                        0.0,
                    )
                    for j in (i, i + 1)
                ]
                at = b * KEYS + i * PIECE
                masks[s, at : at + 2 * PIECE, :] = jnp.concatenate(pieces, axis=0).astype(BF16)

    flip = (((1,), (1,)), ((), ()))
    spans = 2 * len(sets)
    taken = slice(start, start + width)

    def score(s):
        mask(s)
        right = jnp.concatenate([q_refs[s // 2][s % 2, taken, :], one_hot[taken, :]], axis=1)
        best = None
        for b in range(count):
            rows = slice(b * KEYS, (b + 1) * KEYS)
            left = jnp.concatenate([block[b][0, 0:KEYS, :], masks[s, rows, :]], axis=1)
            part = lax.dot_general(left, right, flip, preferred_element_type=F32)
            held[s % 2][rows, :] = part
            peak = jnp.max(part.reshape(KEYS // (8 * GROUP), 8 * GROUP, width), axis=0)
            best = peak if best is None else jnp.maximum(best, peak)
        return best

    best = score(0)
    for s in range(spans):
        top = jnp.max(best, axis=0, keepdims=True)
        at = 2 * sets[0] + s
        if has_state:
            before = state_ref[at, 136:137, taken]
            top = jnp.maximum(before, top)
        for b in range(count):
            rows = slice(b * KEYS, (b + 1) * KEYS)
            weights[s % 2][rows, :] = jnp.exp2((held[s % 2][rows, :] - top) * FACTOR).astype(BF16)
        if s + 1 < spans:
            best = score(s + 1)
        for first in range(0, width, PART):
            inner = slice(first, min(first + PART, width))
            outer = slice(start + inner.start, start + inner.stop)
            sums = jnp.dot(turned[...], weights[s % 2][:, inner], preferred_element_type=F32)[0:136]
            peak = top[:, inner]
            if has_state:
                shrink = jnp.exp2((before[:, inner] - peak) * FACTOR)
                sums = sums + state_ref[at, 0:136, outer] * shrink
            if last:
                pack_state(out_ref, (s,), inner, sums[0:128], sums[128:129], peak)
            else:
                out_ref[s, 0:136, inner] = sums
                out_ref[s, 136:144, inner] = jnp.broadcast_to(peak, (8, peak.shape[1]))


def pack_state(out_ref, lead, cols, weighted, total, top):
    out_ref[(*lead, slice(0, 128), cols)] = weighted.astype(BF16)
    width = top.shape[1]
    line = lax.broadcasted_iota(jnp.int32, (16, width), 0)
    stats = jnp.zeros((16, width), F32)
    for base, value in ((0, top), (3, total)):
        for k in range(3):
            part = value.astype(BF16).astype(F32)
            value = value - part
            stats = jnp.where(line == base + k, jnp.broadcast_to(part, stats.shape), stats)
    out_ref[(*lead, slice(128, 144), cols)] = stats.astype(BF16)


def open_state(ref, lead, cols):
    stats = ref[(*lead, slice(128, 144), cols)].astype(F32)
    top = stats[0:1] + stats[1:2] + stats[2:3]
    total = stats[3:4] + stats[4:5] + stats[5:6]
    return ref[(*lead, slice(0, 128), cols)].astype(F32), total, top


def merge(mine, other):
    top = jnp.maximum(mine[2], other[2])
    a = jnp.exp2((mine[2] - top) * FACTOR)
    b = jnp.exp2((other[2] - top) * FACTOR)
    return mine[0] * a + other[0] * b, mine[1] * a + other[1] * b, top


def read_state(ref, e):
    return ref[e, 0:128, :], ref[e, 128:129, :], ref[e, 136:137, :]


def join_kernel(mine_ref, come_ref, out_ref):
    every = slice(0, COLS // 2)
    for e in range(2):
        merged = merge(read_state(mine_ref, e), open_state(come_ref, (e,), every))
        pack_state(out_ref, (e,), every, *merged)


def finish_kernel(mine_ref, core_ref, plane_ref, out_ref):
    every = slice(0, COLS // 2)
    for e in range(2):
        merged = merge(read_state(mine_ref, e), open_state(core_ref, (e,), every))
        weighted, total, _ = merge(merged, open_state(plane_ref, (e,), every))
        mixed = (weighted / total).T.astype(BF16)
        for h in range(HEADS):
            out_ref[e * SPAN : (e + 1) * SPAN, h * HEAD_DIM : (h + 1) * HEAD_DIM] = mixed[
                h * SPAN : (h + 1) * SPAN
            ]


def attend(stacks, sets, blocks, mine, state, last, start=0, width=COLS):
    count = len(blocks)
    steps = 2 * len(sets)
    keys = KEYS * count
    kernel = functools.partial(
        attend_kernel, mine, sets, start, width, state is not None, last
    )
    args = [stacks[s] for s in sets] + list(blocks)
    if state is not None:
        args.append(state)
    macs = steps * width * keys * (256 + STATE)
    return pl.pallas_call(
        kernel,
        out_shape=jax.ShapeDtypeStruct((steps, STATE, width), BF16 if last else F32),
        scratch_shapes=[
            pltpu.VMEM((STATE, keys), BF16),
            pltpu.VMEM((steps, keys, HEAD_DIM), BF16),
            pltpu.VMEM((COLS, HEAD_DIM), BF16),
            pltpu.VMEM((keys, width), F32),
            pltpu.VMEM((keys, width), F32),
            pltpu.VMEM((keys, width), BF16),
            pltpu.VMEM((keys, width), BF16),
        ],
        compiler_params=pltpu.CompilerParams(vmem_limit_bytes=14 * 1024 * 1024),
        cost_estimate=pl.CostEstimate(
            flops=4 * macs, bytes_accessed=2**20, transcendentals=steps * width * keys
        ),
    )(*args)


def call(kernel, out_shape, *args):
    return pl.pallas_call(
        kernel,
        out_shape=out_shape,
        compiler_params=pltpu.CompilerParams(vmem_limit_bytes=8 * 1024 * 1024),
        cost_estimate=pl.CostEstimate(flops=2**21, bytes_accessed=2**20, transcendentals=0),
    )(*args)


def around(value):
    zs = lax.axis_size("z")
    perm = []
    for z in range(zs):
        perm.append((2 * z, 2 * ((z - 1) % zs)))
        perm.append((2 * z + 1, 2 * ((z + 1) % zs) + 1))
    return lax.ppermute(value, ("z", "core"), perm)


def shifted(value, axis, step):
    size = lax.axis_size(axis)
    return lax.ppermute(value, axis, [(i, (i + step) % size) for i in range(size)])


def ids_to_keys(ids):
    size = {a: lax.axis_size(a) for a in AXES}

    def flat(g, z, x, core):
        return ((g * size["z"] + z) * size["x"] + x) * size["core"] + core

    perm = []
    for g in range(8):
        for z in range(8):
            for core in range(2):
                perm.append((flat(g ^ core, g, z // 2, z % 2), flat(g, z, z // 2, core)))
    return lax.ppermute(ids, AXES, perm)


def body(query_rows, key_rows, value_rows, span_ids):
    ids = jnp.broadcast_to(span_ids.astype(F32)[:, None], (2, HEAD_DIM))
    places = ids_to_keys(ids)
    packed = call(
        pack_kernel,
        jax.ShapeDtypeStruct((4, 4, 56, HEAD_DIM), BF16),
        key_rows,
        value_rows,
        places,
    ).reshape(16, 56, HEAD_DIM)
    routed = lax.all_to_all(packed, ("kv", "x"), 0, 0, tiled=True)
    routed = routed.reshape(4, 4, 56, HEAD_DIM)
    near = call(spread_kernel, jax.ShapeDtypeStruct((1, ROWS, HEAD_DIM), BF16), routed)
    beyond = shifted(query_rows, "pair", 1)
    own = call(
        reorder_kernel, jax.ShapeDtypeStruct((2, COLS // 2, HEAD_DIM), BF16), query_rows
    )
    stack = call(
        stack_kernel,
        jax.ShapeDtypeStruct((2, COLS + 16, HEAD_DIM), BF16),
        own,
        beyond,
        ids,
    )
    stacks = (stack, shifted(stack, "core", 1))
    own_line, other_line = [], []
    own_line.append(around(near))
    mate = shifted(near, "core", 1)
    other_line.append(around(mate))
    for k in range(1, 4):
        own_line.append(around(own_line[-1]))
        if k < 3:
            other_line.append(around(other_line[-1]))
    state = attend(stacks, (0, 1), [near], [True], None, False)
    for k in range(3):
        both = [own_line[k], other_line[k]]
        state = attend(stacks, (0, 1), both, [True, False], state, False)
    far = own_line[3]
    half = COLS // 2
    packed_half = jax.ShapeDtypeStruct((2, STATE, half), BF16)
    leaving = attend(stacks, (1,), [far], [True], state, True, half, half)
    coming = shifted(leaving, "core", 1)
    mine = attend(stacks, (0,), [far], [True], state, False, half, half)
    joined = call(join_kernel, packed_half, mine, coming)
    plane = shifted(joined, "pair", 1)
    leaving = attend(stacks, (1,), [far], [True], state, True, 0, half)
    coming = shifted(leaving, "core", 1)
    mine = attend(stacks, (0,), [far], [True], state, False, 0, half)
    return call(
        finish_kernel,
        jax.ShapeDtypeStruct((2 * SPAN, HEADS * HEAD_DIM), BF16),
        mine,
        coming,
        plane,
    )


def solution(mesh):
    split = Mesh(mesh.devices.reshape(4, 2, 8, 4, 2), AXES)
    groups = ("kv", "pair")
    return jax.shard_map(
        body,
        mesh=split,
        in_specs=(P(BLK, groups), P(groups + BLK, None), P(groups + BLK, None), P(BLK)),
        out_specs=P(BLK, groups),
        check_vma=False,
    )
```

profile of v0, /device:TPU:1, one launch (start us, length us, event | category | flops | bytes accessed | tf_op | source)
XLA Modules:
  0.0 96.1 jit_solution(5632325422877753034)
XLA Ops:
  0.0 0.7 convert_element_type.3
  0.7 0.1 broadcast_in_dim.2.ids_ref
  0.7 5.4 %collective-permute-start.1 = (f32[2,128]{1,0:T(2,128)S(1)}, f32[2,128]{1,0:T(2,128)S(1)}, u32[]{:S(2)}, u32[]{:S(2)}) collective-permute-start(f32[2,128]{1,0:T(2,128)S(1)} %broadcast_in_dim.2.ids_ref), channel_id=1, source_target_pairs={{0,0},{64,1},{1,8},{65,9},{2,18},{66,19},{3,26},{67,27},{4,36},{68... | collective-permute-start | bytes 3080 | tf_op jit(solution)/shard_map/ppermute | solution.py:276
  6.1 0.7 collective-permute-done.1.ids_ref
  6.8 0.0 copy-start.1
  6.8 0.7 copy-done.1
  7.5 0.7 copy-done.2
  8.3 0.7 shard_map.48
  9.0 13.6 %all-to-all-start = ((bf16[16,56,128]{2,1,0:T(8,128)(2,1)}), bf16[16,56,128]{2,1,0:T(8,128)(2,1)S(1)}, u32[]{:S(2)}, u32[]{:S(2)}) async-start(bf16[16,56,128]{2,1,0:T(8,128)(2,1)} %bitcast), calls=%async_computation | async-start | bytes 458752 | tf_op jit(solution)/shard_map/all_to_all | solution.py:289
  22.6 3.0 %collective-permute-start = (bf16[192,512]{1,0:T(8,128)(2,1)}, bf16[192,512]{1,0:T(8,128)(2,1)S(1)}, u32[]{:S(2)}, u32[]{:S(2)}) collective-permute-start(bf16[192,512]{1,0:T(8,128)(2,1)} %source_ref.1), channel_id=1, source_target_pairs={{0,64},{64,0},{1,65},{65,1},{2,66},{66,2},{3,67},{67,3},{4,68},{68... | collective-permute-start | bytes 589832 | tf_op jit(solution)/shard_map/ppermute | solution.py:262
  25.6 0.0 copy-start
  25.6 0.9 copy-done
  26.6 7.2 %collective-permute-done.beyond_ref = bf16[192,512]{1,0:T(8,128)(2,1)S(1)} collective-permute-done((bf16[192,512]{1,0:T(8,128)(2,1)}, bf16[192,512]{1,0:T(8,128)(2,1)S(1)}, u32[]{:S(2)}, u32[]{:S(2)}) %collective-permute-start) | collective-permute-done | bytes 196640 | tf_op jit(solution)/shard_map/ppermute | solution.py:262
  33.9 2.7 %collective-permute-start.6 = (bf16[2,784,128]{2,1,0:T(8,128)(2,1)S(1)}, bf16[2,784,128]{2,1,0:T(8,128)(2,1)S(1)}, u32[]{:S(2)}, u32[]{:S(2)}) collective-permute-start(bf16[2,784,128]{2,1,0:T(8,128)(2,1)S(1)} %shard_map.47.refs_0_), channel_id=1, source_target_pairs={{0,1},{1,0},{2,3},{3,2},{4,5},{5,4},{6,7},{7,6},{8,9},{9,8},{10,11... | collective-permute-start | bytes 1204232 | tf_op jit(solution)/shard_map/ppermute | solution.py:262
  36.5 0.0 all-to-all-done
  36.6 1.9 %collective-permute-start.7 = (bf16[1,784,128]{2,1,0:T(8,128)(2,1)S(1)}, bf16[1,784,128]{2,1,0:T(8,128)(2,1)S(1)}, u32[]{:S(2)}, u32[]{:S(2)}) collective-permute-start(bf16[1,784,128]{2,1,0:T(8,128)(2,1)S(1)} %shard_map.49.refs_2_), channel_id=1, source_target_pairs={{0,1},{1,0},{2,3},{3,2},{4,5},{5,4},{6,7},{7,6},{8,9},{9,8},{10,11... | collective-permute-start | bytes 602120 | tf_op jit(solution)/shard_map/ppermute | solution.py:262
  38.5 2.2 %collective-permute-start.2 = (bf16[1,784,128]{2,1,0:T(8,128)(2,1)S(1)}, bf16[1,784,128]{2,1,0:T(8,128)(2,1)S(1)}, u32[]{:S(2)}, u32[]{:S(2)}) collective-permute-start(bf16[1,784,128]{2,1,0:T(8,128)(2,1)S(1)} %shard_map.49.refs_2_), channel_id=1, source_target_pairs={{0,56},{1,9},{8,0},{9,17},{16,8},{17,25},{24,16},{25,33},{32,24},{... | collective-permute-start | bytes 602120 | tf_op jit(solution)/shard_map/ppermute | solution.py:257
  40.7 0.0 collective-permute-done.7
  40.8 4.0 %collective-permute-start.8 = (bf16[1,784,128]{2,1,0:T(8,128)(2,1)S(1)}, bf16[1,784,128]{2,1,0:T(8,128)(2,1)S(1)}, u32[]{:S(2)}, u32[]{:S(2)}) collective-permute-start(bf16[1,784,128]{2,1,0:T(8,128)(2,1)S(1)} %collective-permute-done.7), channel_id=1, source_target_pairs={{0,56},{1,9},{8,0},{9,17},{16,8},{17,25},{24,16},{25,33},{32,24},{... | collective-permute-start | bytes 602120 | tf_op jit(solution)/shard_map/ppermute | solution.py:257
  44.7 4.4 %collective-permute-done.2.refs_2_ = bf16[1,784,128]{2,1,0:T(8,128)(2,1)S(1)} collective-permute-done((bf16[1,784,128]{2,1,0:T(8,128)(2,1)S(1)}, bf16[1,784,128]{2,1,0:T(8,128)(2,1)S(1)}, u32[]{:S(2)}, u32[]{:S(2)}) %collective-permute-start.2) | collective-permute-done | bytes 200736 | tf_op jit(solution)/shard_map/ppermute | solution.py:257
  49.1 1.9 %collective-permute-start.3 = (bf16[1,784,128]{2,1,0:T(8,128)(2,1)S(1)}, bf16[1,784,128]{2,1,0:T(8,128)(2,1)S(1)}, u32[]{:S(2)}, u32[]{:S(2)}) collective-permute-start(bf16[1,784,128]{2,1,0:T(8,128)(2,1)S(1)} %collective-permute-done.2.refs_2_), channel_id=1, source_target_pairs={{0,56},{1,9},{8,0},{9,17},{16,8},{17,25},{24,16},{25,33},{32,24},{... | collective-permute-start | bytes 602120 | tf_op jit(solution)/shard_map/ppermute | solution.py:257
  51.0 0.0 collective-permute-done.6.refs_1_.refs_0_
  51.0 1.9 %shard_map.50.refs_4_ = f32[4,144,768]{2,1,0:T(8,128)S(1)} custom-call(bf16[2,784,128]{2,1,0:T(8,128)(2,1)S(1)} %shard_map.47.refs_0_, bf16[2,784,128]{2,1,0:T(8,128)(2,1)S(1)} %collective-permute-done.6.refs_1_.refs_0_, bf16[1,784,128]{2,1,0:T(8,128)(2,1)S(1)} %shard_map.49.refs_2_), custom_call_target="tpu_custom_call" | custom-call | flops 1887436800 | bytes 1048576 | tf_op jit(solution)/shard_map/pallas_call | solution.py:223
  53.0 0.0 collective-permute-done.8.refs_3_
  53.0 1.9 %collective-permute-start.9 = (bf16[1,784,128]{2,1,0:T(8,128)(2,1)S(1)}, bf16[1,784,128]{2,1,0:T(8,128)(2,1)S(1)}, u32[]{:S(2)}, u32[]{:S(2)}) collective-permute-start(bf16[1,784,128]{2,1,0:T(8,128)(2,1)S(1)} %collective-permute-done.8.refs_3_), channel_id=1, source_target_pairs={{0,56},{1,9},{8,0},{9,17},{16,8},{17,25},{24,16},{25,33},{32,24},{... | collective-permute-start | bytes 602120 | tf_op jit(solution)/shard_map/ppermute | solution.py:257
  54.9 1.9 %collective-permute-done.3.refs_2_ = bf16[1,784,128]{2,1,0:T(8,128)(2,1)S(1)} collective-permute-done((bf16[1,784,128]{2,1,0:T(8,128)(2,1)S(1)}, bf16[1,784,128]{2,1,0:T(8,128)(2,1)S(1)}, u32[]{:S(2)}, u32[]{:S(2)}) %collective-permute-start.3) | collective-permute-done | bytes 200736 | tf_op jit(solution)/shard_map/ppermute | solution.py:257
  56.8 1.9 %collective-permute-start.4 = (bf16[1,784,128]{2,1,0:T(8,128)(2,1)S(1)}, bf16[1,784,128]{2,1,0:T(8,128)(2,1)S(1)}, u32[]{:S(2)}, u32[]{:S(2)}) collective-permute-start(bf16[1,784,128]{2,1,0:T(8,128)(2,1)S(1)} %collective-permute-done.3.refs_2_), channel_id=1, source_target_pairs={{0,56},{1,9},{8,0},{9,17},{16,8},{17,25},{24,16},{25,33},{32,24},{... | collective-permute-start | bytes 602120 | tf_op jit(solution)/shard_map/ppermute | solution.py:257
  58.7 3.6 %shard_map.51.refs_4_ = f32[4,144,768]{2,1,0:T(8,128)S(1)} custom-call(bf16[2,784,128]{2,1,0:T(8,128)(2,1)S(1)} %shard_map.47.refs_0_, bf16[2,784,128]{2,1,0:T(8,128)(2,1)S(1)} %collective-permute-done.6.refs_1_.refs_0_, bf16[1,784,128]{2,1,0:T(8,128)(2,1)S(1)} %collective-permute-done.2.refs_2_, bf16[1,784,128]{2,1,0:T(8,128)(2,1)S(1)} %collective-permute-done.8.refs_3_, ...), custom_call_target="tpu_custom_call" | custom-call | flops 3774873600 | bytes 1048576 | tf_op jit(solution)/shard_map/pallas_call | solution.py:223
  62.3 0.0 collective-permute-done.9.refs_3_
  62.3 2.7 %collective-permute-start.10 = (bf16[1,784,128]{2,1,0:T(8,128)(2,1)S(1)}, bf16[1,784,128]{2,1,0:T(8,128)(2,1)S(1)}, u32[]{:S(2)}, u32[]{:S(2)}) collective-permute-start(bf16[1,784,128]{2,1,0:T(8,128)(2,1)S(1)} %collective-permute-done.9.refs_3_), channel_id=1, source_target_pairs={{0,56},{1,9},{8,0},{9,17},{16,8},{17,25},{24,16},{25,33},{32,24},{... | collective-permute-start | bytes 602120 | tf_op jit(solution)/shard_map/ppermute | solution.py:257
  65.0 0.0 collective-permute-done.4.refs_2_
  65.0 2.7 %collective-permute-start.5 = (bf16[1,784,128]{2,1,0:T(8,128)(2,1)S(1)}, bf16[1,784,128]{2,1,0:T(8,128)(2,1)S(1)}, u32[]{:S(2)}, u32[]{:S(2)}) collective-permute-start(bf16[1,784,128]{2,1,0:T(8,128)(2,1)S(1)} %collective-permute-done.4.refs_2_), channel_id=1, source_target_pairs={{0,56},{1,9},{8,0},{9,17},{16,8},{17,25},{24,16},{25,33},{32,24},{... | collective-permute-start | bytes 602120 | tf_op jit(solution)/shard_map/ppermute | solution.py:257
  67.7 3.6 %shard_map.52.refs_4_ = f32[4,144,768]{2,1,0:T(8,128)S(1)} custom-call(bf16[2,784,128]{2,1,0:T(8,128)(2,1)S(1)} %shard_map.47.refs_0_, bf16[2,784,128]{2,1,0:T(8,128)(2,1)S(1)} %collective-permute-done.6.refs_1_.refs_0_, bf16[1,784,128]{2,1,0:T(8,128)(2,1)S(1)} %collective-permute-done.3.refs_2_, bf16[1,784,128]{2,1,0:T(8,128)(2,1)S(1)} %collective-permute-done.9.refs_3_, ...), custom_call_target="tpu_custom_call" | custom-call | flops 3774873600 | bytes 1048576 | tf_op jit(solution)/shard_map/pallas_call | solution.py:223
  71.3 0.0 collective-permute-done.10.refs_3_
  71.3 3.6 %shard_map.53.refs_2_ = f32[4,144,768]{2,1,0:T(8,128)S(1)} custom-call(bf16[2,784,128]{2,1,0:T(8,128)(2,1)S(1)} %shard_map.47.refs_0_, bf16[2,784,128]{2,1,0:T(8,128)(2,1)S(1)} %collective-permute-done.6.refs_1_.refs_0_, bf16[1,784,128]{2,1,0:T(8,128)(2,1)S(1)} %collective-permute-done.4.refs_2_, bf16[1,784,128]{2,1,0:T(8,128)(2,1)S(1)} %collective-permute-done.10.refs_3_, ...), custom_call_target="tpu_custom_call" | custom-call | flops 3774873600 | bytes 1048576 | tf_op jit(solution)/shard_map/pallas_call | solution.py:223
  74.9 0.0 collective-permute-done.5.refs_1_
  74.9 0.9 shard_map.57
  75.8 7.2 %collective-permute-start.12 = (bf16[2,144,384]{2,1,0:T(8,128)(2,1)S(1)}, bf16[2,144,384]{2,1,0:T(8,128)(2,1)S(1)}, u32[]{:S(2)}, u32[]{:S(2)}) collective-permute-start(bf16[2,144,384]{2,1,0:T(8,128)(2,1)S(1)} %shard_map.57), channel_id=1, source_target_pairs={{0,1},{1,0},{2,3},{3,2},{4,5},{5,4},{6,7},{7,6},{8,9},{9,8},{10,11... | collective-permute-start | bytes 663560 | tf_op jit(solution)/shard_map/ppermute | solution.py:262
  83.0 0.9 shard_map.55
  83.9 1.9 %collective-permute-start.11 = (bf16[2,144,384]{2,1,0:T(8,128)(2,1)S(1)}, bf16[2,144,384]{2,1,0:T(8,128)(2,1)S(1)}, u32[]{:S(2)}, u32[]{:S(2)}) collective-permute-start(bf16[2,144,384]{2,1,0:T(8,128)(2,1)S(1)} %shard_map.55), channel_id=1, source_target_pairs={{0,1},{1,0},{2,3},{3,2},{4,5},{5,4},{6,7},{7,6},{8,9},{9,8},{10,11... | collective-permute-start | bytes 663560 | tf_op jit(solution)/shard_map/ppermute | solution.py:262
  85.8 0.8 shard_map.56.mine_ref
  86.6 0.0 collective-permute-done.12.come_ref
  86.6 0.1 shard_map.58
  86.8 3.2 %collective-permute-start.13 = (bf16[2,144,384]{2,1,0:T(8,128)(2,1)S(1)}, bf16[2,144,384]{2,1,0:T(8,128)(2,1)S(1)}, u32[]{:S(2)}, u32[]{:S(2)}) collective-permute-start(bf16[2,144,384]{2,1,0:T(8,128)(2,1)S(1)} %shard_map.58), channel_id=1, source_target_pairs={{0,64},{64,0},{1,65},{65,1},{2,66},{66,2},{3,67},{67,3},{4,68},{68... | collective-permute-start | bytes 663560 | tf_op jit(solution)/shard_map/ppermute | solution.py:262
  89.9 0.8 shard_map.54.mine_ref
  90.8 0.0 collective-permute-done.11.core_ref
  90.8 4.4 %collective-permute-done.13.plane_ref = bf16[2,144,384]{2,1,0:T(8,128)(2,1)S(1)} collective-permute-done((bf16[2,144,384]{2,1,0:T(8,128)(2,1)S(1)}, bf16[2,144,384]{2,1,0:T(8,128)(2,1)S(1)}, u32[]{:S(2)}, u32[]{:S(2)}) %collective-permute-start.13) | collective-permute-done | bytes 221216 | tf_op jit(solution)/shard_map/ppermute | solution.py:262
  95.2 0.9 shard_map.59
  (4 shorter events, 0.1 us)
Async XLA Ops:
  0.7 6.1 %collective-permute-start.1 = (f32[2,128]{1,0:T(2,128)S(1)}, f32[2,128]{1,0:T(2,128)S(1)}, u32[]{:S(2)}, u32[]{:S(2)}) collective-permute-start(f32[2,128]{1,0:T(2,128)S(1)} %broadcast_in_dim.2.ids_ref), channel_id=1, source_target_pairs={{0,0},{64,1},{1,8},{65,9},{2,18},{66,19},{3,26},{67,27},{4,36},{68... | collective-permute-start | bytes 3080 | tf_op jit(solution)/shard_map/ppermute | solution.py:276
  6.8 0.7 copy-start.1
  7.5 0.7 copy-start.2
  9.0 27.5 %all-to-all-start = ((bf16[16,56,128]{2,1,0:T(8,128)(2,1)}), bf16[16,56,128]{2,1,0:T(8,128)(2,1)S(1)}, u32[]{:S(2)}, u32[]{:S(2)}) async-start(bf16[16,56,128]{2,1,0:T(8,128)(2,1)} %bitcast), calls=%async_computation | async-start | bytes 458752 | tf_op jit(solution)/shard_map/all_to_all | solution.py:289
  22.6 11.2 %collective-permute-start = (bf16[192,512]{1,0:T(8,128)(2,1)}, bf16[192,512]{1,0:T(8,128)(2,1)S(1)}, u32[]{:S(2)}, u32[]{:S(2)}) collective-permute-start(bf16[192,512]{1,0:T(8,128)(2,1)} %source_ref.1), channel_id=1, source_target_pairs={{0,64},{64,0},{1,65},{65,1},{2,66},{66,2},{3,67},{67,3},{4,68},{68... | collective-permute-start | bytes 589832 | tf_op jit(solution)/shard_map/ppermute | solution.py:262
  25.6 0.9 copy-start
  33.9 17.2 %collective-permute-start.6 = (bf16[2,784,128]{2,1,0:T(8,128)(2,1)S(1)}, bf16[2,784,128]{2,1,0:T(8,128)(2,1)S(1)}, u32[]{:S(2)}, u32[]{:S(2)}) collective-permute-start(bf16[2,784,128]{2,1,0:T(8,128)(2,1)S(1)} %shard_map.47.refs_0_), channel_id=1, source_target_pairs={{0,1},{1,0},{2,3},{3,2},{4,5},{5,4},{6,7},{7,6},{8,9},{9,8},{10,11... | collective-permute-start | bytes 1204232 | tf_op jit(solution)/shard_map/ppermute | solution.py:262
  36.6 4.2 %collective-permute-start.7 = (bf16[1,784,128]{2,1,0:T(8,128)(2,1)S(1)}, bf16[1,784,128]{2,1,0:T(8,128)(2,1)S(1)}, u32[]{:S(2)}, u32[]{:S(2)}) collective-permute-start(bf16[1,784,128]{2,1,0:T(8,128)(2,1)S(1)} %shard_map.49.refs_2_), channel_id=1, source_target_pairs={{0,1},{1,0},{2,3},{3,2},{4,5},{5,4},{6,7},{7,6},{8,9},{9,8},{10,11... | collective-permute-start | bytes 602120 | tf_op jit(solution)/shard_map/ppermute | solution.py:262
  38.5 10.6 %collective-permute-start.2 = (bf16[1,784,128]{2,1,0:T(8,128)(2,1)S(1)}, bf16[1,784,128]{2,1,0:T(8,128)(2,1)S(1)}, u32[]{:S(2)}, u32[]{:S(2)}) collective-permute-start(bf16[1,784,128]{2,1,0:T(8,128)(2,1)S(1)} %shard_map.49.refs_2_), channel_id=1, source_target_pairs={{0,56},{1,9},{8,0},{9,17},{16,8},{17,25},{24,16},{25,33},{32,24},{... | collective-permute-start | bytes 602120 | tf_op jit(solution)/shard_map/ppermute | solution.py:257
  40.8 12.2 %collective-permute-start.8 = (bf16[1,784,128]{2,1,0:T(8,128)(2,1)S(1)}, bf16[1,784,128]{2,1,0:T(8,128)(2,1)S(1)}, u32[]{:S(2)}, u32[]{:S(2)}) collective-permute-start(bf16[1,784,128]{2,1,0:T(8,128)(2,1)S(1)} %collective-permute-done.7), channel_id=1, source_target_pairs={{0,56},{1,9},{8,0},{9,17},{16,8},{17,25},{24,16},{25,33},{32,24},{... | collective-permute-start | bytes 602120 | tf_op jit(solution)/shard_map/ppermute | solution.py:257
  49.1 7.7 %collective-permute-start.3 = (bf16[1,784,128]{2,1,0:T(8,128)(2,1)S(1)}, bf16[1,784,128]{2,1,0:T(8,128)(2,1)S(1)}, u32[]{:S(2)}, u32[]{:S(2)}) collective-permute-start(bf16[1,784,128]{2,1,0:T(8,128)(2,1)S(1)} %collective-permute-done.2.refs_2_), channel_id=1, source_target_pairs={{0,56},{1,9},{8,0},{9,17},{16,8},{17,25},{24,16},{25,33},{32,24},{... | collective-permute-start | bytes 602120 | tf_op jit(solution)/shard_map/ppermute | solution.py:257
  53.0 9.3 %collective-permute-start.9 = (bf16[1,784,128]{2,1,0:T(8,128)(2,1)S(1)}, bf16[1,784,128]{2,1,0:T(8,128)(2,1)S(1)}, u32[]{:S(2)}, u32[]{:S(2)}) collective-permute-start(bf16[1,784,128]{2,1,0:T(8,128)(2,1)S(1)} %collective-permute-done.8.refs_3_), channel_id=1, source_target_pairs={{0,56},{1,9},{8,0},{9,17},{16,8},{17,25},{24,16},{25,33},{32,24},{... | collective-permute-start | bytes 602120 | tf_op jit(solution)/shard_map/ppermute | solution.py:257
  56.8 8.2 %collective-permute-start.4 = (bf16[1,784,128]{2,1,0:T(8,128)(2,1)S(1)}, bf16[1,784,128]{2,1,0:T(8,128)(2,1)S(1)}, u32[]{:S(2)}, u32[]{:S(2)}) collective-permute-start(bf16[1,784,128]{2,1,0:T(8,128)(2,1)S(1)} %collective-permute-done.3.refs_2_), channel_id=1, source_target_pairs={{0,56},{1,9},{8,0},{9,17},{16,8},{17,25},{24,16},{25,33},{32,24},{... | collective-permute-start | bytes 602120 | tf_op jit(solution)/shard_map/ppermute | solution.py:257
  62.3 9.0 %collective-permute-start.10 = (bf16[1,784,128]{2,1,0:T(8,128)(2,1)S(1)}, bf16[1,784,128]{2,1,0:T(8,128)(2,1)S(1)}, u32[]{:S(2)}, u32[]{:S(2)}) collective-permute-start(bf16[1,784,128]{2,1,0:T(8,128)(2,1)S(1)} %collective-permute-done.9.refs_3_), channel_id=1, source_target_pairs={{0,56},{1,9},{8,0},{9,17},{16,8},{17,25},{24,16},{25,33},{32,24},{... | collective-permute-start | bytes 602120 | tf_op jit(solution)/shard_map/ppermute | solution.py:257
  65.0 9.9 %collective-permute-start.5 = (bf16[1,784,128]{2,1,0:T(8,128)(2,1)S(1)}, bf16[1,784,128]{2,1,0:T(8,128)(2,1)S(1)}, u32[]{:S(2)}, u32[]{:S(2)}) collective-permute-start(bf16[1,784,128]{2,1,0:T(8,128)(2,1)S(1)} %collective-permute-done.4.refs_2_), channel_id=1, source_target_pairs={{0,56},{1,9},{8,0},{9,17},{16,8},{17,25},{24,16},{25,33},{32,24},{... | collective-permute-start | bytes 602120 | tf_op jit(solution)/shard_map/ppermute | solution.py:257
  75.8 10.9 %collective-permute-start.12 = (bf16[2,144,384]{2,1,0:T(8,128)(2,1)S(1)}, bf16[2,144,384]{2,1,0:T(8,128)(2,1)S(1)}, u32[]{:S(2)}, u32[]{:S(2)}) collective-permute-start(bf16[2,144,384]{2,1,0:T(8,128)(2,1)S(1)} %shard_map.57), channel_id=1, source_target_pairs={{0,1},{1,0},{2,3},{3,2},{4,5},{5,4},{6,7},{7,6},{8,9},{9,8},{10,11... | collective-permute-start | bytes 663560 | tf_op jit(solution)/shard_map/ppermute | solution.py:262
  83.9 6.9 %collective-permute-start.11 = (bf16[2,144,384]{2,1,0:T(8,128)(2,1)S(1)}, bf16[2,144,384]{2,1,0:T(8,128)(2,1)S(1)}, u32[]{:S(2)}, u32[]{:S(2)}) collective-permute-start(bf16[2,144,384]{2,1,0:T(8,128)(2,1)S(1)} %shard_map.55), channel_id=1, source_target_pairs={{0,1},{1,0},{2,3},{3,2},{4,5},{5,4},{6,7},{7,6},{8,9},{9,8},{10,11... | collective-permute-start | bytes 663560 | tf_op jit(solution)/shard_map/ppermute | solution.py:262
  86.8 8.4 %collective-permute-start.13 = (bf16[2,144,384]{2,1,0:T(8,128)(2,1)S(1)}, bf16[2,144,384]{2,1,0:T(8,128)(2,1)S(1)}, u32[]{:S(2)}, u32[]{:S(2)}) collective-permute-start(bf16[2,144,384]{2,1,0:T(8,128)(2,1)S(1)} %shard_map.58), channel_id=1, source_target_pairs={{0,64},{64,0},{1,65},{65,1},{2,66},{66,2},{3,67},{67,3},{4,68},{68... | collective-permute-start | bytes 663560 | tf_op jit(solution)/shard_map/ppermute | solution.py:262
where the time goes:
time: 97.2 us; the launch traced here: 96.1 us
  starting transfers between devices  56.2 us (58%)
  waiting for transfers between devices  18.5 us (19%)
  Pallas kernels  18 us (19%)
  local copies, waits for them, and re-layouts  2.48 us (3%)
    ppermute x6, starting transfers between devices, shifted(): lax.ppermute(value, axis, [(i, (i + step) % size) for i in range(size)])  19.9 us
    ppermute x7, starting transfers between devices, around(): return lax.ppermute(value, ('z', 'core'), perm)  17.3 us
    pallas_call x8, Pallas kernels, attend(): pl.pallas_call(kernel, out_shape=jax.ShapeDtypeStruct((steps, STATE, widt...  16.1 us
    all_to_all x1, starting transfers between devices, body(): routed = lax.all_to_all(packed, ('kv', 'x'), 0, 0, tiled=True)  13.6 us
    ppermute x6, waiting for transfers between devices, shifted(): lax.ppermute(value, axis, [(i, (i + step) % size) for i in range(size)])  11.6 us
    ppermute x7, waiting for transfers between devices, around(): return lax.ppermute(value, ('z', 'core'), perm)  6.25 us
    ppermute x1, starting transfers between devices, ids_to_keys(): return lax.ppermute(ids, AXES, perm)  5.37 us
    unnamed x6, local copies, waits for them, and re-layouts  2.4 us
  transfers between devices with their start and end apart: 15, of which 5 were waited for; matrix products, arithmetic and copies ran while one was open for 0% of the time, Pallas kernels for 16%

commit v1 on v0

--- a/solution.py
+++ b/solution.py
@@ -309,10 +309,15 @@
         own_line.append(around(own_line[-1]))
         if k < 3:
             other_line.append(around(other_line[-1]))
-    state = attend(stacks, (0, 1), [near], [True], None, False)
-    for k in range(3):
-        both = [own_line[k], other_line[k]]
-        state = attend(stacks, (0, 1), both, [True, False], state, False)
+    state = None
+    parts = [
+        ([near, own_line[0]], [True, True]),
+        ([other_line[0], own_line[1]], [False, True]),
+        ([other_line[1], own_line[2]], [False, True]),
+        ([other_line[2]], [False]),
+    ]
+    for blocks, mine in parts:
+        state = attend(stacks, (0, 1), blocks, mine, state, False)
     far = own_line[3]
     half = COLS // 2
     packed_half = jax.ShapeDtypeStruct((2, STATE, half), BF16)

time: 97.2 us -> 97.5 us (level)
  starting transfers between devices: 56.2 us -> 61.5 us
  waiting for transfers between devices: 18.5 us -> 13.8 us
    ppermute x7, waiting for transfers between devices: 6.25 us -> 1.09 us  [around(): return lax.ppermute(value, ('z', 'core'), perm)]
    ppermute x6, starting transfers between devices: 19.9 us -> 24.6 us  [shifted(): lax.ppermute(value, axis, [(i, (i + step) % size) for i in range(size)])]
  transfers between devices with their start and end apart: 15 -> 15, of which waited for: 5 -> 6; matrix products, arithmetic and copies ran while one was open for 0% -> 0% of each run, Pallas kernels for 16% -> 16%
where the time goes in v1:
time: 97.5 us; the launch traced here: 96.8 us
  starting transfers between devices  61.5 us (63%)
  Pallas kernels  18.1 us (19%)
  waiting for transfers between devices  13.8 us (14%)
  local copies, waits for them, and re-layouts  2.48 us (3%)
    ppermute x6, starting transfers between devices, shifted(): lax.ppermute(value, axis, [(i, (i + step) % size) for i in range(size)])  24.6 us
    ppermute x7, starting transfers between devices, around(): return lax.ppermute(value, ('z', 'core'), perm)  17.9 us
    pallas_call x8, Pallas kernels, attend(): pl.pallas_call(kernel, out_shape=jax.ShapeDtypeStruct((steps, STATE, widt...  16.2 us
    all_to_all x1, starting transfers between devices, body(): routed = lax.all_to_all(packed, ('kv', 'x'), 0, 0, tiled=True)  13.6 us
    ppermute x6, waiting for transfers between devices, shifted(): lax.ppermute(value, axis, [(i, (i + step) % size) for i in range(size)])  12 us
    ppermute x1, starting transfers between devices, ids_to_keys(): return lax.ppermute(ids, AXES, perm)  5.37 us
    unnamed x6, local copies, waits for them, and re-layouts  2.4 us
  transfers between devices with their start and end apart: 15, of which 6 were waited for; matrix products, arithmetic and copies ran while one was open for 0% of the time, Pallas kernels for 16%

profile of v1, /device:TPU:1, one launch (start us, length us, event | category | flops | bytes accessed | tf_op | source)
XLA Modules:
  0.0 96.8 jit_solution(14948233828665055442)
XLA Ops:
  0.0 0.7 convert_element_type.3
  0.7 0.1 broadcast_in_dim.2.ids_ref
  0.7 5.4 %collective-permute-start.1 = (f32[2,128]{1,0:T(2,128)S(1)}, f32[2,128]{1,0:T(2,128)S(1)}, u32[]{:S(2)}, u32[]{:S(2)}) collective-permute-start(f32[2,128]{1,0:T(2,128)S(1)} %broadcast_in_dim.2.ids_ref), channel_id=1, source_target_pairs={{0,0},{64,1},{1,8},{65,9},{2,18},{66,19},{3,26},{67,27},{4,36},{68... | collective-permute-start | bytes 3080 | tf_op jit(solution)/shard_map/ppermute | solution.py:276
  6.1 0.7 collective-permute-done.1.ids_ref
  6.8 0.0 copy-start.1
  6.8 0.7 copy-done.1
  7.5 0.7 copy-done.2
  8.3 0.7 shard_map.48
  9.0 13.6 %all-to-all-start = ((bf16[16,56,128]{2,1,0:T(8,128)(2,1)}), bf16[16,56,128]{2,1,0:T(8,128)(2,1)S(1)}, u32[]{:S(2)}, u32[]{:S(2)}) async-start(bf16[16,56,128]{2,1,0:T(8,128)(2,1)} %bitcast), calls=%async_computation | async-start | bytes 458752 | tf_op jit(solution)/shard_map/all_to_all | solution.py:289
  22.6 3.0 %collective-permute-start = (bf16[192,512]{1,0:T(8,128)(2,1)}, bf16[192,512]{1,0:T(8,128)(2,1)S(1)}, u32[]{:S(2)}, u32[]{:S(2)}) collective-permute-start(bf16[192,512]{1,0:T(8,128)(2,1)} %source_ref.1), channel_id=1, source_target_pairs={{0,64},{64,0},{1,65},{65,1},{2,66},{66,2},{3,67},{67,3},{4,68},{68... | collective-permute-start | bytes 589832 | tf_op jit(solution)/shard_map/ppermute | solution.py:262
  25.6 0.0 copy-start
  25.6 0.9 copy-done
  26.6 7.2 %collective-permute-done.beyond_ref = bf16[192,512]{1,0:T(8,128)(2,1)S(1)} collective-permute-done((bf16[192,512]{1,0:T(8,128)(2,1)}, bf16[192,512]{1,0:T(8,128)(2,1)S(1)}, u32[]{:S(2)}, u32[]{:S(2)}) %collective-permute-start) | collective-permute-done | bytes 196640 | tf_op jit(solution)/shard_map/ppermute | solution.py:262
  33.9 2.7 %collective-permute-start.6 = (bf16[2,784,128]{2,1,0:T(8,128)(2,1)S(1)}, bf16[2,784,128]{2,1,0:T(8,128)(2,1)S(1)}, u32[]{:S(2)}, u32[]{:S(2)}) collective-permute-start(bf16[2,784,128]{2,1,0:T(8,128)(2,1)S(1)} %shard_map.47.refs_0_), channel_id=1, source_target_pairs={{0,1},{1,0},{2,3},{3,2},{4,5},{5,4},{6,7},{7,6},{8,9},{9,8},{10,11... | collective-permute-start | bytes 1204232 | tf_op jit(solution)/shard_map/ppermute | solution.py:262
  36.5 0.0 all-to-all-done
  36.6 2.2 %collective-permute-start.2 = (bf16[1,784,128]{2,1,0:T(8,128)(2,1)S(1)}, bf16[1,784,128]{2,1,0:T(8,128)(2,1)S(1)}, u32[]{:S(2)}, u32[]{:S(2)}) collective-permute-start(bf16[1,784,128]{2,1,0:T(8,128)(2,1)S(1)} %shard_map.49.refs_2_), channel_id=1, source_target_pairs={{0,56},{1,9},{8,0},{9,17},{16,8},{17,25},{24,16},{25,33},{32,24},{... | collective-permute-start | bytes 602120 | tf_op jit(solution)/shard_map/ppermute | solution.py:257
  38.8 7.5 %collective-permute-start.7 = (bf16[1,784,128]{2,1,0:T(8,128)(2,1)S(1)}, bf16[1,784,128]{2,1,0:T(8,128)(2,1)S(1)}, u32[]{:S(2)}, u32[]{:S(2)}) collective-permute-start(bf16[1,784,128]{2,1,0:T(8,128)(2,1)S(1)} %shard_map.49.refs_2_), channel_id=1, source_target_pairs={{0,1},{1,0},{2,3},{3,2},{4,5},{5,4},{6,7},{7,6},{8,9},{9,8},{10,11... | collective-permute-start | bytes 602120 | tf_op jit(solution)/shard_map/ppermute | solution.py:262
  46.3 0.5 collective-permute-done.2.refs_3_
  46.8 1.9 %collective-permute-start.3 = (bf16[1,784,128]{2,1,0:T(8,128)(2,1)S(1)}, bf16[1,784,128]{2,1,0:T(8,128)(2,1)S(1)}, u32[]{:S(2)}, u32[]{:S(2)}) collective-permute-start(bf16[1,784,128]{2,1,0:T(8,128)(2,1)S(1)} %collective-permute-done.2.refs_3_), channel_id=1, source_target_pairs={{0,56},{1,9},{8,0},{9,17},{16,8},{17,25},{24,16},{25,33},{32,24},{... | collective-permute-start | bytes 602120 | tf_op jit(solution)/shard_map/ppermute | solution.py:257
  48.7 0.0 collective-permute-done.7
  48.7 1.9 %collective-permute-start.8 = (bf16[1,784,128]{2,1,0:T(8,128)(2,1)S(1)}, bf16[1,784,128]{2,1,0:T(8,128)(2,1)S(1)}, u32[]{:S(2)}, u32[]{:S(2)}) collective-permute-start(bf16[1,784,128]{2,1,0:T(8,128)(2,1)S(1)} %collective-permute-done.7), channel_id=1, source_target_pairs={{0,56},{1,9},{8,0},{9,17},{16,8},{17,25},{24,16},{25,33},{32,24},{... | collective-permute-start | bytes 602120 | tf_op jit(solution)/shard_map/ppermute | solution.py:257
  50.7 0.0 collective-permute-done.6.refs_1_.refs_0_
  50.7 3.4 %shard_map.50.refs_4_ = f32[4,144,768]{2,1,0:T(8,128)S(1)} custom-call(bf16[2,784,128]{2,1,0:T(8,128)(2,1)S(1)} %shard_map.47.refs_0_, bf16[2,784,128]{2,1,0:T(8,128)(2,1)S(1)} %collective-permute-done.6.refs_1_.refs_0_, bf16[1,784,128]{2,1,0:T(8,128)(2,1)S(1)} %shard_map.49.refs_2_, bf16[1,784,128]{2,1,0:T(8,128)(2,1)S(1)} %collective-permute-done.2.refs_3_), custom_call_target="tpu_custom_call" | custom-call | flops 3774873600 | bytes 1048576 | tf_op jit(solution)/shard_map/pallas_call | solution.py:223
  54.1 0.4 collective-permute-done.3.refs_3_
  54.5 1.9 %collective-permute-start.4 = (bf16[1,784,128]{2,1,0:T(8,128)(2,1)S(1)}, bf16[1,784,128]{2,1,0:T(8,128)(2,1)S(1)}, u32[]{:S(2)}, u32[]{:S(2)}) collective-permute-start(bf16[1,784,128]{2,1,0:T(8,128)(2,1)S(1)} %collective-permute-done.3.refs_3_), channel_id=1, source_target_pairs={{0,56},{1,9},{8,0},{9,17},{16,8},{17,25},{24,16},{25,33},{32,24},{... | collective-permute-start | bytes 602120 | tf_op jit(solution)/shard_map/ppermute | solution.py:257
  56.4 0.2 collective-permute-done.8.refs_2_
  56.6 4.4 %collective-permute-start.9 = (bf16[1,784,128]{2,1,0:T(8,128)(2,1)S(1)}, bf16[1,784,128]{2,1,0:T(8,128)(2,1)S(1)}, u32[]{:S(2)}, u32[]{:S(2)}) collective-permute-start(bf16[1,784,128]{2,1,0:T(8,128)(2,1)S(1)} %collective-permute-done.8.refs_2_), channel_id=1, source_target_pairs={{0,56},{1,9},{8,0},{9,17},{16,8},{17,25},{24,16},{25,33},{32,24},{... | collective-permute-start | bytes 602120 | tf_op jit(solution)/shard_map/ppermute | solution.py:257
  61.0 3.6 %shard_map.51.refs_4_ = f32[4,144,768]{2,1,0:T(8,128)S(1)} custom-call(bf16[2,784,128]{2,1,0:T(8,128)(2,1)S(1)} %shard_map.47.refs_0_, bf16[2,784,128]{2,1,0:T(8,128)(2,1)S(1)} %collective-permute-done.6.refs_1_.refs_0_, bf16[1,784,128]{2,1,0:T(8,128)(2,1)S(1)} %collective-permute-done.8.refs_2_, bf16[1,784,128]{2,1,0:T(8,128)(2,1)S(1)} %collective-permute-done.3.refs_3_, ...), custom_call_target="tpu_custom_call" | custom-call | flops 3774873600 | bytes 1048576 | tf_op jit(solution)/shard_map/pallas_call | solution.py:223
  64.6 0.0 collective-permute-done.9.refs_2_
  64.6 3.1 %collective-permute-start.10 = (bf16[1,784,128]{2,1,0:T(8,128)(2,1)S(1)}, bf16[1,784,128]{2,1,0:T(8,128)(2,1)S(1)}, u32[]{:S(2)}, u32[]{:S(2)}) collective-permute-start(bf16[1,784,128]{2,1,0:T(8,128)(2,1)S(1)} %collective-permute-done.9.refs_2_), channel_id=1, source_target_pairs={{0,56},{1,9},{8,0},{9,17},{16,8},{17,25},{24,16},{25,33},{32,24},{... | collective-permute-start | bytes 602120 | tf_op jit(solution)/shard_map/ppermute | solution.py:257
  67.7 0.0 collective-permute-done.4.refs_3_
  67.7 2.4 %collective-permute-start.5 = (bf16[1,784,128]{2,1,0:T(8,128)(2,1)S(1)}, bf16[1,784,128]{2,1,0:T(8,128)(2,1)S(1)}, u32[]{:S(2)}, u32[]{:S(2)}) collective-permute-start(bf16[1,784,128]{2,1,0:T(8,128)(2,1)S(1)} %collective-permute-done.4.refs_3_), channel_id=1, source_target_pairs={{0,56},{1,9},{8,0},{9,17},{16,8},{17,25},{24,16},{25,33},{32,24},{... | collective-permute-start | bytes 602120 | tf_op jit(solution)/shard_map/ppermute | solution.py:257
  70.2 3.6 %shard_map.52.refs_3_ = f32[4,144,768]{2,1,0:T(8,128)S(1)} custom-call(bf16[2,784,128]{2,1,0:T(8,128)(2,1)S(1)} %shard_map.47.refs_0_, bf16[2,784,128]{2,1,0:T(8,128)(2,1)S(1)} %collective-permute-done.6.refs_1_.refs_0_, bf16[1,784,128]{2,1,0:T(8,128)(2,1)S(1)} %collective-permute-done.9.refs_2_, bf16[1,784,128]{2,1,0:T(8,128)(2,1)S(1)} %collective-permute-done.4.refs_3_, ...), custom_call_target="tpu_custom_call" | custom-call | flops 3774873600 | bytes 1048576 | tf_op jit(solution)/shard_map/pallas_call | solution.py:223
  73.8 0.0 collective-permute-done.10.refs_2_
  73.8 2.2 %shard_map.53.refs_2_ = f32[4,144,768]{2,1,0:T(8,128)S(1)} custom-call(bf16[2,784,128]{2,1,0:T(8,128)(2,1)S(1)} %shard_map.47.refs_0_, bf16[2,784,128]{2,1,0:T(8,128)(2,1)S(1)} %collective-permute-done.6.refs_1_.refs_0_, bf16[1,784,128]{2,1,0:T(8,128)(2,1)S(1)} %collective-permute-done.10.refs_2_, f32[4,144,768]{2,1,0:T(8,128)S(1)} %shard_map.52.refs_3_), custom_call_target="tpu_custom_call" | custom-call | flops 1887436800 | bytes 1048576 | tf_op jit(solution)/shard_map/pallas_call | solution.py:223
  76.0 0.0 collective-permute-done.5.refs_1_
  76.0 0.8 shard_map.57
  76.9 6.8 %collective-permute-start.12 = (bf16[2,144,384]{2,1,0:T(8,128)(2,1)S(1)}, bf16[2,144,384]{2,1,0:T(8,128)(2,1)S(1)}, u32[]{:S(2)}, u32[]{:S(2)}) collective-permute-start(bf16[2,144,384]{2,1,0:T(8,128)(2,1)S(1)} %shard_map.57), channel_id=1, source_target_pairs={{0,1},{1,0},{2,3},{3,2},{4,5},{5,4},{6,7},{7,6},{8,9},{9,8},{10,11... | collective-permute-start | bytes 663560 | tf_op jit(solution)/shard_map/ppermute | solution.py:262
  83.7 0.9 shard_map.55
  84.5 1.9 %collective-permute-start.11 = (bf16[2,144,384]{2,1,0:T(8,128)(2,1)S(1)}, bf16[2,144,384]{2,1,0:T(8,128)(2,1)S(1)}, u32[]{:S(2)}, u32[]{:S(2)}) collective-permute-start(bf16[2,144,384]{2,1,0:T(8,128)(2,1)S(1)} %shard_map.55), channel_id=1, source_target_pairs={{0,1},{1,0},{2,3},{3,2},{4,5},{5,4},{6,7},{7,6},{8,9},{9,8},{10,11... | collective-permute-start | bytes 663560 | tf_op jit(solution)/shard_map/ppermute | solution.py:262
  86.5 0.8 shard_map.56.mine_ref
  87.3 0.0 collective-permute-done.12.come_ref
  87.3 0.1 shard_map.58
  87.5 2.8 %collective-permute-start.13 = (bf16[2,144,384]{2,1,0:T(8,128)(2,1)S(1)}, bf16[2,144,384]{2,1,0:T(8,128)(2,1)S(1)}, u32[]{:S(2)}, u32[]{:S(2)}) collective-permute-start(bf16[2,144,384]{2,1,0:T(8,128)(2,1)S(1)} %shard_map.58), channel_id=1, source_target_pairs={{0,64},{64,0},{1,65},{65,1},{2,66},{66,2},{3,67},{67,3},{4,68},{68... | collective-permute-start | bytes 663560 | tf_op jit(solution)/shard_map/ppermute | solution.py:262
  90.2 0.8 shard_map.54.mine_ref
  91.1 0.0 collective-permute-done.11.core_ref
  91.1 4.8 %collective-permute-done.13.plane_ref = bf16[2,144,384]{2,1,0:T(8,128)(2,1)S(1)} collective-permute-done((bf16[2,144,384]{2,1,0:T(8,128)(2,1)S(1)}, bf16[2,144,384]{2,1,0:T(8,128)(2,1)S(1)}, u32[]{:S(2)}, u32[]{:S(2)}) %collective-permute-start.13) | collective-permute-done | bytes 221216 | tf_op jit(solution)/shard_map/ppermute | solution.py:262
  95.8 0.9 shard_map.59
  (4 shorter events, 0.1 us)
Async XLA Ops:
  0.7 6.1 %collective-permute-start.1 = (f32[2,128]{1,0:T(2,128)S(1)}, f32[2,128]{1,0:T(2,128)S(1)}, u32[]{:S(2)}, u32[]{:S(2)}) collective-permute-start(f32[2,128]{1,0:T(2,128)S(1)} %broadcast_in_dim.2.ids_ref), channel_id=1, source_target_pairs={{0,0},{64,1},{1,8},{65,9},{2,18},{66,19},{3,26},{67,27},{4,36},{68... | collective-permute-start | bytes 3080 | tf_op jit(solution)/shard_map/ppermute | solution.py:276
  6.8 0.7 copy-start.1
  7.5 0.7 copy-start.2
  9.0 27.5 %all-to-all-start = ((bf16[16,56,128]{2,1,0:T(8,128)(2,1)}), bf16[16,56,128]{2,1,0:T(8,128)(2,1)S(1)}, u32[]{:S(2)}, u32[]{:S(2)}) async-start(bf16[16,56,128]{2,1,0:T(8,128)(2,1)} %bitcast), calls=%async_computation | async-start | bytes 458752 | tf_op jit(solution)/shard_map/all_to_all | solution.py:289
  22.6 11.2 %collective-permute-start = (bf16[192,512]{1,0:T(8,128)(2,1)}, bf16[192,512]{1,0:T(8,128)(2,1)S(1)}, u32[]{:S(2)}, u32[]{:S(2)}) collective-permute-start(bf16[192,512]{1,0:T(8,128)(2,1)} %source_ref.1), channel_id=1, source_target_pairs={{0,64},{64,0},{1,65},{65,1},{2,66},{66,2},{3,67},{67,3},{4,68},{68... | collective-permute-start | bytes 589832 | tf_op jit(solution)/shard_map/ppermute | solution.py:262
  25.6 0.9 copy-start
  33.9 16.8 %collective-permute-start.6 = (bf16[2,784,128]{2,1,0:T(8,128)(2,1)S(1)}, bf16[2,784,128]{2,1,0:T(8,128)(2,1)S(1)}, u32[]{:S(2)}, u32[]{:S(2)}) collective-permute-start(bf16[2,784,128]{2,1,0:T(8,128)(2,1)S(1)} %shard_map.47.refs_0_), channel_id=1, source_target_pairs={{0,1},{1,0},{2,3},{3,2},{4,5},{5,4},{6,7},{7,6},{8,9},{9,8},{10,11... | collective-permute-start | bytes 1204232 | tf_op jit(solution)/shard_map/ppermute | solution.py:262
  36.6 10.2 %collective-permute-start.2 = (bf16[1,784,128]{2,1,0:T(8,128)(2,1)S(1)}, bf16[1,784,128]{2,1,0:T(8,128)(2,1)S(1)}, u32[]{:S(2)}, u32[]{:S(2)}) collective-permute-start(bf16[1,784,128]{2,1,0:T(8,128)(2,1)S(1)} %shard_map.49.refs_2_), channel_id=1, source_target_pairs={{0,56},{1,9},{8,0},{9,17},{16,8},{17,25},{24,16},{25,33},{32,24},{... | collective-permute-start | bytes 602120 | tf_op jit(solution)/shard_map/ppermute | solution.py:257
  38.8 9.9 %collective-permute-start.7 = (bf16[1,784,128]{2,1,0:T(8,128)(2,1)S(1)}, bf16[1,784,128]{2,1,0:T(8,128)(2,1)S(1)}, u32[]{:S(2)}, u32[]{:S(2)}) collective-permute-start(bf16[1,784,128]{2,1,0:T(8,128)(2,1)S(1)} %shard_map.49.refs_2_), channel_id=1, source_target_pairs={{0,1},{1,0},{2,3},{3,2},{4,5},{5,4},{6,7},{7,6},{8,9},{9,8},{10,11... | collective-permute-start | bytes 602120 | tf_op jit(solution)/shard_map/ppermute | solution.py:262
  46.8 7.7 %collective-permute-start.3 = (bf16[1,784,128]{2,1,0:T(8,128)(2,1)S(1)}, bf16[1,784,128]{2,1,0:T(8,128)(2,1)S(1)}, u32[]{:S(2)}, u32[]{:S(2)}) collective-permute-start(bf16[1,784,128]{2,1,0:T(8,128)(2,1)S(1)} %collective-permute-done.2.refs_3_), channel_id=1, source_target_pairs={{0,56},{1,9},{8,0},{9,17},{16,8},{17,25},{24,16},{25,33},{32,24},{... | collective-permute-start | bytes 602120 | tf_op jit(solution)/shard_map/ppermute | solution.py:257
  48.7 7.9 %collective-permute-start.8 = (bf16[1,784,128]{2,1,0:T(8,128)(2,1)S(1)}, bf16[1,784,128]{2,1,0:T(8,128)(2,1)S(1)}, u32[]{:S(2)}, u32[]{:S(2)}) collective-permute-start(bf16[1,784,128]{2,1,0:T(8,128)(2,1)S(1)} %collective-permute-done.7), channel_id=1, source_target_pairs={{0,56},{1,9},{8,0},{9,17},{16,8},{17,25},{24,16},{25,33},{32,24},{... | collective-permute-start | bytes 602120 | tf_op jit(solution)/shard_map/ppermute | solution.py:257
  54.5 13.3 %collective-permute-start.4 = (bf16[1,784,128]{2,1,0:T(8,128)(2,1)S(1)}, bf16[1,784,128]{2,1,0:T(8,128)(2,1)S(1)}, u32[]{:S(2)}, u32[]{:S(2)}) collective-permute-start(bf16[1,784,128]{2,1,0:T(8,128)(2,1)S(1)} %collective-permute-done.3.refs_3_), channel_id=1, source_target_pairs={{0,56},{1,9},{8,0},{9,17},{16,8},{17,25},{24,16},{25,33},{32,24},{... | collective-permute-start | bytes 602120 | tf_op jit(solution)/shard_map/ppermute | solution.py:257
  56.6 8.0 %collective-permute-start.9 = (bf16[1,784,128]{2,1,0:T(8,128)(2,1)S(1)}, bf16[1,784,128]{2,1,0:T(8,128)(2,1)S(1)}, u32[]{:S(2)}, u32[]{:S(2)}) collective-permute-start(bf16[1,784,128]{2,1,0:T(8,128)(2,1)S(1)} %collective-permute-done.8.refs_2_), channel_id=1, source_target_pairs={{0,56},{1,9},{8,0},{9,17},{16,8},{17,25},{24,16},{25,33},{32,24},{... | collective-permute-start | bytes 602120 | tf_op jit(solution)/shard_map/ppermute | solution.py:257
  64.6 9.2 %collective-permute-start.10 = (bf16[1,784,128]{2,1,0:T(8,128)(2,1)S(1)}, bf16[1,784,128]{2,1,0:T(8,128)(2,1)S(1)}, u32[]{:S(2)}, u32[]{:S(2)}) collective-permute-start(bf16[1,784,128]{2,1,0:T(8,128)(2,1)S(1)} %collective-permute-done.9.refs_2_), channel_id=1, source_target_pairs={{0,56},{1,9},{8,0},{9,17},{16,8},{17,25},{24,16},{25,33},{32,24},{... | collective-permute-start | bytes 602120 | tf_op jit(solution)/shard_map/ppermute | solution.py:257
  67.7 8.3 %collective-permute-start.5 = (bf16[1,784,128]{2,1,0:T(8,128)(2,1)S(1)}, bf16[1,784,128]{2,1,0:T(8,128)(2,1)S(1)}, u32[]{:S(2)}, u32[]{:S(2)}) collective-permute-start(bf16[1,784,128]{2,1,0:T(8,128)(2,1)S(1)} %collective-permute-done.4.refs_3_), channel_id=1, source_target_pairs={{0,56},{1,9},{8,0},{9,17},{16,8},{17,25},{24,16},{25,33},{32,24},{... | collective-permute-start | bytes 602120 | tf_op jit(solution)/shard_map/ppermute | solution.py:257
  76.9 10.5 %collective-permute-start.12 = (bf16[2,144,384]{2,1,0:T(8,128)(2,1)S(1)}, bf16[2,144,384]{2,1,0:T(8,128)(2,1)S(1)}, u32[]{:S(2)}, u32[]{:S(2)}) collective-permute-start(bf16[2,144,384]{2,1,0:T(8,128)(2,1)S(1)} %shard_map.57), channel_id=1, source_target_pairs={{0,1},{1,0},{2,3},{3,2},{4,5},{5,4},{6,7},{7,6},{8,9},{9,8},{10,11... | collective-permute-start | bytes 663560 | tf_op jit(solution)/shard_map/ppermute | solution.py:262
  84.5 6.5 %collective-permute-start.11 = (bf16[2,144,384]{2,1,0:T(8,128)(2,1)S(1)}, bf16[2,144,384]{2,1,0:T(8,128)(2,1)S(1)}, u32[]{:S(2)}, u32[]{:S(2)}) collective-permute-start(bf16[2,144,384]{2,1,0:T(8,128)(2,1)S(1)} %shard_map.55), channel_id=1, source_target_pairs={{0,1},{1,0},{2,3},{3,2},{4,5},{5,4},{6,7},{7,6},{8,9},{9,8},{10,11... | collective-permute-start | bytes 663560 | tf_op jit(solution)/shard_map/ppermute | solution.py:262
  87.5 8.4 %collective-permute-start.13 = (bf16[2,144,384]{2,1,0:T(8,128)(2,1)S(1)}, bf16[2,144,384]{2,1,0:T(8,128)(2,1)S(1)}, u32[]{:S(2)}, u32[]{:S(2)}) collective-permute-start(bf16[2,144,384]{2,1,0:T(8,128)(2,1)S(1)} %shard_map.58), channel_id=1, source_target_pairs={{0,64},{64,0},{1,65},{65,1},{2,66},{66,2},{3,67},{67,3},{4,68},{68... | collective-permute-start | bytes 663560 | tf_op jit(solution)/shard_map/ppermute | solution.py:262

commit v2 on v1

--- a/solution.py
+++ b/solution.py
@@ -28,8 +28,13 @@
 BF16 = jnp.bfloat16
 
 
+def id_rows(ids_ref, rows):
+    line = lax.broadcasted_iota(jnp.int32, (rows, HEAD_DIM), 0)
+    return jnp.where(line % 2 == 0, ids_ref[0], ids_ref[1]).astype(F32).astype(BF16)
+
+
 def pack_kernel(key_ref, value_ref, ids_ref, out_ref):
-    own = jnp.concatenate([ids_ref[...]] * 4, axis=0).astype(BF16)
+    own = id_rows(ids_ref, 8)
     for head in range(4):
         lanes = slice(head * HEAD_DIM, (head + 1) * HEAD_DIM)
         for x in range(4):
@@ -65,7 +70,7 @@
 
 
 def stack_kernel(own_ref, beyond_ref, ids_ref, out_ref):
-    ids = jnp.concatenate([ids_ref[...]] * 8, axis=0).astype(BF16)
+    ids = id_rows(ids_ref, 16)
     reorder(beyond_ref, out_ref, COLS // 2)
     for e in range(2):
         out_ref[e, 0 : COLS // 2, :] = own_ref[e]
@@ -240,8 +245,10 @@
 
 
 def call(kernel, out_shape, *args):
+    spaces = [pltpu.SMEM if arg.dtype == jnp.int32 else pltpu.VMEM for arg in args]
     return pl.pallas_call(
         kernel,
+        in_specs=[pl.BlockSpec(memory_space=space) for space in spaces],
         out_shape=out_shape,
         compiler_params=pltpu.CompilerParams(vmem_limit_bytes=8 * 1024 * 1024),
         cost_estimate=pl.CostEstimate(flops=2**21, bytes_accessed=2**20, transcendentals=0),
@@ -277,8 +284,7 @@
 
 
 def body(query_rows, key_rows, value_rows, span_ids):
-    ids = jnp.broadcast_to(span_ids.astype(F32)[:, None], (2, HEAD_DIM))
-    places = ids_to_keys(ids)
+    places = ids_to_keys(span_ids)
     packed = call(
         pack_kernel,
         jax.ShapeDtypeStruct((4, 4, 56, HEAD_DIM), BF16),
@@ -298,7 +304,7 @@
         jax.ShapeDtypeStruct((2, COLS + 16, HEAD_DIM), BF16),
         own,
         beyond,
-        ids,
+        span_ids,
     )
     stacks = (stack, shifted(stack, "core", 1))
     own_line, other_line = [], []

time: 97.5 us -> 98.6 us (1.011)
  Pallas kernels: 18.1 us -> 19.1 us
    pallas_call x6, Pallas kernels: 1.88 us -> 2.94 us  [call(): pl.pallas_call(kernel, in_specs=[pl.BlockSpec(memory_space=space) for spa...]
    unnamed x6 -> x8, local copies, waits for them, and re-layouts: 2.4 us -> 3.06 us
  transfers between devices with their start and end apart: 15 -> 15, of which waited for: 6 -> 6; matrix products, arithmetic and copies ran while one was open for 0% -> 0% of each run, Pallas kernels for 16% -> 17%
where the time goes in v2:
time: 98.6 us; the launch traced here: 97.5 us
  starting transfers between devices  61.1 us (62%)
  Pallas kernels  19.1 us (19%)
  waiting for transfers between devices  13.9 us (14%)
  local copies, waits for them, and re-layouts  3.06 us (3%)
    ppermute x6, starting transfers between devices, shifted(): lax.ppermute(value, axis, [(i, (i + step) % size) for i in range(size)])  24.3 us
    ppermute x7, starting transfers between devices, around(): return lax.ppermute(value, ('z', 'core'), perm)  17.9 us
    pallas_call x8, Pallas kernels, attend(): pl.pallas_call(kernel, out_shape=jax.ShapeDtypeStruct((steps, STATE, widt...  16.2 us
    all_to_all x1, starting transfers between devices, body(): routed = lax.all_to_all(packed, ('kv', 'x'), 0, 0, tiled=True)  13.6 us
    ppermute x6, waiting for transfers between devices, shifted(): lax.ppermute(value, axis, [(i, (i + step) % size) for i in range(size)])  11.6 us
    ppermute x1, starting transfers between devices, ids_to_keys(): return lax.ppermute(ids, AXES, perm)  5.37 us
    unnamed x8, local copies, waits for them, and re-layouts  3.06 us
    pallas_call x6, Pallas kernels, call(): pl.pallas_call(kernel, in_specs=[pl.BlockSpec(memory_space=space) for spa...  2.94 us
  transfers between devices with their start and end apart: 15, of which 6 were waited for; matrix products, arithmetic and copies ran while one was open for 0% of the time, Pallas kernels for 17%

profile of v2, /device:TPU:1, one launch (start us, length us, event | category | flops | bytes accessed | tf_op | source)
XLA Modules:
  0.0 97.5 jit_solution(8451948829894169523)
XLA Ops:
  0.0 5.4 %collective-permute-start.1 = (s32[2]{0:T(128)}, s32[2]{0:T(128)S(1)}, u32[]{:S(2)}, u32[]{:S(2)}) collective-permute-start(s32[2]{0:T(128)} %ids_ref.1), channel_id=1, source_target_pairs={{0,0},{64,1},{1,8},{65,9},{2,18},{66,19},{3,26},{67,27},{4,36},{68... | collective-permute-start | bytes 32 | tf_op jit(solution)/shard_map/ppermute | solution.py:283
  5.4 0.8 collective-permute-done.1.ids_ref
  6.2 0.0 copy-start.1
  6.2 0.7 copy-done.1
  7.0 0.7 copy-done.2
  7.7 1.2 %shard_map.48 = bf16[4,4,56,128]{3,2,1,0:T(8,128)(2,1)} custom-call(bf16[24,512]{1,0:T(8,128)(2,1)S(1)} %copy-done.1, bf16[24,512]{1,0:T(8,128)(2,1)S(1)} %copy-done.2, s32[2]{0:T(128)S(1)} %collective-permute-done.1.ids_ref), custom_call_target="tpu_custom_call" | custom-call | flops 2097152 | bytes 1048576 | tf_op jit(solution)/shard_map/pallas_call | solution.py:249
  8.9 13.6 %all-to-all-start = ((bf16[16,56,128]{2,1,0:T(8,128)(2,1)}), bf16[16,56,128]{2,1,0:T(8,128)(2,1)S(1)}, u32[]{:S(2)}, u32[]{:S(2)}) async-start(bf16[16,56,128]{2,1,0:T(8,128)(2,1)} %bitcast), calls=%async_computation | async-start | bytes 458752 | tf_op jit(solution)/shard_map/all_to_all | solution.py:295
  22.5 3.0 %collective-permute-start = (bf16[192,512]{1,0:T(8,128)(2,1)}, bf16[192,512]{1,0:T(8,128)(2,1)S(1)}, u32[]{:S(2)}, u32[]{:S(2)}) collective-permute-start(bf16[192,512]{1,0:T(8,128)(2,1)} %source_ref.1), channel_id=1, source_target_pairs={{0,64},{64,0},{1,65},{65,1},{2,66},{66,2},{3,67},{67,3},{4,68},{68... | collective-permute-start | bytes 589832 | tf_op jit(solution)/shard_map/ppermute | solution.py:269
  25.5 0.0 copy-start
  25.5 0.9 copy-done
  26.5 7.2 %collective-permute-done.beyond_ref = bf16[192,512]{1,0:T(8,128)(2,1)S(1)} collective-permute-done((bf16[192,512]{1,0:T(8,128)(2,1)}, bf16[192,512]{1,0:T(8,128)(2,1)S(1)}, u32[]{:S(2)}, u32[]{:S(2)}) %collective-permute-start) | collective-permute-done | bytes 196640 | tf_op jit(solution)/shard_map/ppermute | solution.py:269
  33.7 0.7 copy-done.3
  34.4 0.6 shard_map.47.refs_0_
  35.0 2.7 %collective-permute-start.6 = (bf16[2,784,128]{2,1,0:T(8,128)(2,1)S(1)}, bf16[2,784,128]{2,1,0:T(8,128)(2,1)S(1)}, u32[]{:S(2)}, u32[]{:S(2)}) collective-permute-start(bf16[2,784,128]{2,1,0:T(8,128)(2,1)S(1)} %shard_map.47.refs_0_), channel_id=1, source_target_pairs={{0,1},{1,0},{2,3},{3,2},{4,5},{5,4},{6,7},{7,6},{8,9},{9,8},{10,11... | collective-permute-start | bytes 1204232 | tf_op jit(solution)/shard_map/ppermute | solution.py:269
  37.7 0.0 all-to-all-done
  37.7 2.2 %collective-permute-start.2 = (bf16[1,784,128]{2,1,0:T(8,128)(2,1)S(1)}, bf16[1,784,128]{2,1,0:T(8,128)(2,1)S(1)}, u32[]{:S(2)}, u32[]{:S(2)}) collective-permute-start(bf16[1,784,128]{2,1,0:T(8,128)(2,1)S(1)} %shard_map.49.refs_2_), channel_id=1, source_target_pairs={{0,56},{1,9},{8,0},{9,17},{16,8},{17,25},{24,16},{25,33},{32,24},{... | collective-permute-start | bytes 602120 | tf_op jit(solution)/shard_map/ppermute | solution.py:264
  39.9 7.1 %collective-permute-start.7 = (bf16[1,784,128]{2,1,0:T(8,128)(2,1)S(1)}, bf16[1,784,128]{2,1,0:T(8,128)(2,1)S(1)}, u32[]{:S(2)}, u32[]{:S(2)}) collective-permute-start(bf16[1,784,128]{2,1,0:T(8,128)(2,1)S(1)} %shard_map.49.refs_2_), channel_id=1, source_target_pairs={{0,1},{1,0},{2,3},{3,2},{4,5},{5,4},{6,7},{7,6},{8,9},{9,8},{10,11... | collective-permute-start | bytes 602120 | tf_op jit(solution)/shard_map/ppermute | solution.py:269
  47.1 0.9 collective-permute-done.2.refs_3_
  47.9 1.9 %collective-permute-start.3 = (bf16[1,784,128]{2,1,0:T(8,128)(2,1)S(1)}, bf16[1,784,128]{2,1,0:T(8,128)(2,1)S(1)}, u32[]{:S(2)}, u32[]{:S(2)}) collective-permute-start(bf16[1,784,128]{2,1,0:T(8,128)(2,1)S(1)} %collective-permute-done.2.refs_3_), channel_id=1, source_target_pairs={{0,56},{1,9},{8,0},{9,17},{16,8},{17,25},{24,16},{25,33},{32,24},{... | collective-permute-start | bytes 602120 | tf_op jit(solution)/shard_map/ppermute | solution.py:264
  49.9 0.0 collective-permute-done.7
  49.9 1.9 %collective-permute-start.8 = (bf16[1,784,128]{2,1,0:T(8,128)(2,1)S(1)}, bf16[1,784,128]{2,1,0:T(8,128)(2,1)S(1)}, u32[]{:S(2)}, u32[]{:S(2)}) collective-permute-start(bf16[1,784,128]{2,1,0:T(8,128)(2,1)S(1)} %collective-permute-done.7), channel_id=1, source_target_pairs={{0,56},{1,9},{8,0},{9,17},{16,8},{17,25},{24,16},{25,33},{32,24},{... | collective-permute-start | bytes 602120 | tf_op jit(solution)/shard_map/ppermute | solution.py:264
  51.8 0.0 collective-permute-done.6.refs_1_.refs_0_
  51.8 3.4 %shard_map.50.refs_4_ = f32[4,144,768]{2,1,0:T(8,128)S(1)} custom-call(bf16[2,784,128]{2,1,0:T(8,128)(2,1)S(1)} %shard_map.47.refs_0_, bf16[2,784,128]{2,1,0:T(8,128)(2,1)S(1)} %collective-permute-done.6.refs_1_.refs_0_, bf16[1,784,128]{2,1,0:T(8,128)(2,1)S(1)} %shard_map.49.refs_2_, bf16[1,784,128]{2,1,0:T(8,128)(2,1)S(1)} %collective-permute-done.2.refs_3_), custom_call_target="tpu_custom_call" | custom-call | flops 3774873600 | bytes 1048576 | tf_op jit(solution)/shard_map/pallas_call | solution.py:228
  55.2 0.4 collective-permute-done.3.refs_3_
  55.6 1.9 %collective-permute-start.4 = (bf16[1,784,128]{2,1,0:T(8,128)(2,1)S(1)}, bf16[1,784,128]{2,1,0:T(8,128)(2,1)S(1)}, u32[]{:S(2)}, u32[]{:S(2)}) collective-permute-start(bf16[1,784,128]{2,1,0:T(8,128)(2,1)S(1)} %collective-permute-done.3.refs_3_), channel_id=1, source_target_pairs={{0,56},{1,9},{8,0},{9,17},{16,8},{17,25},{24,16},{25,33},{32,24},{... | collective-permute-start | bytes 602120 | tf_op jit(solution)/shard_map/ppermute | solution.py:264
  57.5 0.2 collective-permute-done.8.refs_2_
  57.7 4.4 %collective-permute-start.9 = (bf16[1,784,128]{2,1,0:T(8,128)(2,1)S(1)}, bf16[1,784,128]{2,1,0:T(8,128)(2,1)S(1)}, u32[]{:S(2)}, u32[]{:S(2)}) collective-permute-start(bf16[1,784,128]{2,1,0:T(8,128)(2,1)S(1)} %collective-permute-done.8.refs_2_), channel_id=1, source_target_pairs={{0,56},{1,9},{8,0},{9,17},{16,8},{17,25},{24,16},{25,33},{32,24},{... | collective-permute-start | bytes 602120 | tf_op jit(solution)/shard_map/ppermute | solution.py:264
  62.1 3.6 %shard_map.51.refs_4_ = f32[4,144,768]{2,1,0:T(8,128)S(1)} custom-call(bf16[2,784,128]{2,1,0:T(8,128)(2,1)S(1)} %shard_map.47.refs_0_, bf16[2,784,128]{2,1,0:T(8,128)(2,1)S(1)} %collective-permute-done.6.refs_1_.refs_0_, bf16[1,784,128]{2,1,0:T(8,128)(2,1)S(1)} %collective-permute-done.8.refs_2_, bf16[1,784,128]{2,1,0:T(8,128)(2,1)S(1)} %collective-permute-done.3.refs_3_, ...), custom_call_target="tpu_custom_call" | custom-call | flops 3774873600 | bytes 1048576 | tf_op jit(solution)/shard_map/pallas_call | solution.py:228
  65.7 0.0 collective-permute-done.9.refs_2_
  65.7 3.1 %collective-permute-start.10 = (bf16[1,784,128]{2,1,0:T(8,128)(2,1)S(1)}, bf16[1,784,128]{2,1,0:T(8,128)(2,1)S(1)}, u32[]{:S(2)}, u32[]{:S(2)}) collective-permute-start(bf16[1,784,128]{2,1,0:T(8,128)(2,1)S(1)} %collective-permute-done.9.refs_2_), channel_id=1, source_target_pairs={{0,56},{1,9},{8,0},{9,17},{16,8},{17,25},{24,16},{25,33},{32,24},{... | collective-permute-start | bytes 602120 | tf_op jit(solution)/shard_map/ppermute | solution.py:264
  68.9 0.0 collective-permute-done.4.refs_3_
  68.9 2.4 %collective-permute-start.5 = (bf16[1,784,128]{2,1,0:T(8,128)(2,1)S(1)}, bf16[1,784,128]{2,1,0:T(8,128)(2,1)S(1)}, u32[]{:S(2)}, u32[]{:S(2)}) collective-permute-start(bf16[1,784,128]{2,1,0:T(8,128)(2,1)S(1)} %collective-permute-done.4.refs_3_), channel_id=1, source_target_pairs={{0,56},{1,9},{8,0},{9,17},{16,8},{17,25},{24,16},{25,33},{32,24},{... | collective-permute-start | bytes 602120 | tf_op jit(solution)/shard_map/ppermute | solution.py:264
  71.3 3.6 %shard_map.52.refs_3_ = f32[4,144,768]{2,1,0:T(8,128)S(1)} custom-call(bf16[2,784,128]{2,1,0:T(8,128)(2,1)S(1)} %shard_map.47.refs_0_, bf16[2,784,128]{2,1,0:T(8,128)(2,1)S(1)} %collective-permute-done.6.refs_1_.refs_0_, bf16[1,784,128]{2,1,0:T(8,128)(2,1)S(1)} %collective-permute-done.9.refs_2_, bf16[1,784,128]{2,1,0:T(8,128)(2,1)S(1)} %collective-permute-done.4.refs_3_, ...), custom_call_target="tpu_custom_call" | custom-call | flops 3774873600 | bytes 1048576 | tf_op jit(solution)/shard_map/pallas_call | solution.py:228
  74.9 0.0 collective-permute-done.10.refs_2_
  74.9 2.2 %shard_map.53.refs_2_ = f32[4,144,768]{2,1,0:T(8,128)S(1)} custom-call(bf16[2,784,128]{2,1,0:T(8,128)(2,1)S(1)} %shard_map.47.refs_0_, bf16[2,784,128]{2,1,0:T(8,128)(2,1)S(1)} %collective-permute-done.6.refs_1_.refs_0_, bf16[1,784,128]{2,1,0:T(8,128)(2,1)S(1)} %collective-permute-done.10.refs_2_, f32[4,144,768]{2,1,0:T(8,128)S(1)} %shard_map.52.refs_3_), custom_call_target="tpu_custom_call" | custom-call | flops 1887436800 | bytes 1048576 | tf_op jit(solution)/shard_map/pallas_call | solution.py:228
  77.1 0.0 collective-permute-done.5.refs_1_
  77.1 0.8 shard_map.57
  78.0 6.4 %collective-permute-start.12 = (bf16[2,144,384]{2,1,0:T(8,128)(2,1)S(1)}, bf16[2,144,384]{2,1,0:T(8,128)(2,1)S(1)}, u32[]{:S(2)}, u32[]{:S(2)}) collective-permute-start(bf16[2,144,384]{2,1,0:T(8,128)(2,1)S(1)} %shard_map.57), channel_id=1, source_target_pairs={{0,1},{1,0},{2,3},{3,2},{4,5},{5,4},{6,7},{7,6},{8,9},{9,8},{10,11... | collective-permute-start | bytes 663560 | tf_op jit(solution)/shard_map/ppermute | solution.py:269
  84.4 0.8 shard_map.55
  85.3 1.9 %collective-permute-start.11 = (bf16[2,144,384]{2,1,0:T(8,128)(2,1)S(1)}, bf16[2,144,384]{2,1,0:T(8,128)(2,1)S(1)}, u32[]{:S(2)}, u32[]{:S(2)}) collective-permute-start(bf16[2,144,384]{2,1,0:T(8,128)(2,1)S(1)} %shard_map.55), channel_id=1, source_target_pairs={{0,1},{1,0},{2,3},{3,2},{4,5},{5,4},{6,7},{7,6},{8,9},{9,8},{10,11... | collective-permute-start | bytes 663560 | tf_op jit(solution)/shard_map/ppermute | solution.py:269
  87.2 0.8 shard_map.56.mine_ref
  88.0 0.0 collective-permute-done.12.come_ref
  88.0 0.1 shard_map.58
  88.2 3.2 %collective-permute-start.13 = (bf16[2,144,384]{2,1,0:T(8,128)(2,1)S(1)}, bf16[2,144,384]{2,1,0:T(8,128)(2,1)S(1)}, u32[]{:S(2)}, u32[]{:S(2)}) collective-permute-start(bf16[2,144,384]{2,1,0:T(8,128)(2,1)S(1)} %shard_map.58), channel_id=1, source_target_pairs={{0,64},{64,0},{1,65},{65,1},{2,66},{66,2},{3,67},{67,3},{4,68},{68... | collective-permute-start | bytes 663560 | tf_op jit(solution)/shard_map/ppermute | solution.py:269
  91.3 0.8 shard_map.54.mine_ref
  92.2 0.0 collective-permute-done.11.core_ref
  92.2 4.4 %collective-permute-done.13.plane_ref = bf16[2,144,384]{2,1,0:T(8,128)(2,1)S(1)} collective-permute-done((bf16[2,144,384]{2,1,0:T(8,128)(2,1)S(1)}, bf16[2,144,384]{2,1,0:T(8,128)(2,1)S(1)}, u32[]{:S(2)}, u32[]{:S(2)}) %collective-permute-start.13) | collective-permute-done | bytes 221216 | tf_op jit(solution)/shard_map/ppermute | solution.py:269
  96.6 0.9 shard_map.59
  (4 shorter events, 0.1 us)
Async XLA Ops:
  0.0 6.2 %collective-permute-start.1 = (s32[2]{0:T(128)}, s32[2]{0:T(128)S(1)}, u32[]{:S(2)}, u32[]{:S(2)}) collective-permute-start(s32[2]{0:T(128)} %ids_ref.1), channel_id=1, source_target_pairs={{0,0},{64,1},{1,8},{65,9},{2,18},{66,19},{3,26},{67,27},{4,36},{68... | collective-permute-start | bytes 32 | tf_op jit(solution)/shard_map/ppermute | solution.py:283
  6.2 0.7 copy-start.1
  6.9 0.7 copy-start.2
  8.9 28.7 %all-to-all-start = ((bf16[16,56,128]{2,1,0:T(8,128)(2,1)}), bf16[16,56,128]{2,1,0:T(8,128)(2,1)S(1)}, u32[]{:S(2)}, u32[]{:S(2)}) async-start(bf16[16,56,128]{2,1,0:T(8,128)(2,1)} %bitcast), calls=%async_computation | async-start | bytes 458752 | tf_op jit(solution)/shard_map/all_to_all | solution.py:295
  22.5 11.2 %collective-permute-start = (bf16[192,512]{1,0:T(8,128)(2,1)}, bf16[192,512]{1,0:T(8,128)(2,1)S(1)}, u32[]{:S(2)}, u32[]{:S(2)}) collective-permute-start(bf16[192,512]{1,0:T(8,128)(2,1)} %source_ref.1), channel_id=1, source_target_pairs={{0,64},{64,0},{1,65},{65,1},{2,66},{66,2},{3,67},{67,3},{4,68},{68... | collective-permute-start | bytes 589832 | tf_op jit(solution)/shard_map/ppermute | solution.py:269
  25.5 0.9 copy-start
  33.7 0.7 copy-start.3
  35.0 16.8 %collective-permute-start.6 = (bf16[2,784,128]{2,1,0:T(8,128)(2,1)S(1)}, bf16[2,784,128]{2,1,0:T(8,128)(2,1)S(1)}, u32[]{:S(2)}, u32[]{:S(2)}) collective-permute-start(bf16[2,784,128]{2,1,0:T(8,128)(2,1)S(1)} %shard_map.47.refs_0_), channel_id=1, source_target_pairs={{0,1},{1,0},{2,3},{3,2},{4,5},{5,4},{6,7},{7,6},{8,9},{9,8},{10,11... | collective-permute-start | bytes 1204232 | tf_op jit(solution)/shard_map/ppermute | solution.py:269
  37.7 10.2 %collective-permute-start.2 = (bf16[1,784,128]{2,1,0:T(8,128)(2,1)S(1)}, bf16[1,784,128]{2,1,0:T(8,128)(2,1)S(1)}, u32[]{:S(2)}, u32[]{:S(2)}) collective-permute-start(bf16[1,784,128]{2,1,0:T(8,128)(2,1)S(1)} %shard_map.49.refs_2_), channel_id=1, source_target_pairs={{0,56},{1,9},{8,0},{9,17},{16,8},{17,25},{24,16},{25,33},{32,24},{... | collective-permute-start | bytes 602120 | tf_op jit(solution)/shard_map/ppermute | solution.py:264
  39.9 9.9 %collective-permute-start.7 = (bf16[1,784,128]{2,1,0:T(8,128)(2,1)S(1)}, bf16[1,784,128]{2,1,0:T(8,128)(2,1)S(1)}, u32[]{:S(2)}, u32[]{:S(2)}) collective-permute-start(bf16[1,784,128]{2,1,0:T(8,128)(2,1)S(1)} %shard_map.49.refs_2_), channel_id=1, source_target_pairs={{0,1},{1,0},{2,3},{3,2},{4,5},{5,4},{6,7},{7,6},{8,9},{9,8},{10,11... | collective-permute-start | bytes 602120 | tf_op jit(solution)/shard_map/ppermute | solution.py:269
  47.9 7.7 %collective-permute-start.3 = (bf16[1,784,128]{2,1,0:T(8,128)(2,1)S(1)}, bf16[1,784,128]{2,1,0:T(8,128)(2,1)S(1)}, u32[]{:S(2)}, u32[]{:S(2)}) collective-permute-start(bf16[1,784,128]{2,1,0:T(8,128)(2,1)S(1)} %collective-permute-done.2.refs_3_), channel_id=1, source_target_pairs={{0,56},{1,9},{8,0},{9,17},{16,8},{17,25},{24,16},{25,33},{32,24},{... | collective-permute-start | bytes 602120 | tf_op jit(solution)/shard_map/ppermute | solution.py:264
  49.9 7.9 %collective-permute-start.8 = (bf16[1,784,128]{2,1,0:T(8,128)(2,1)S(1)}, bf16[1,784,128]{2,1,0:T(8,128)(2,1)S(1)}, u32[]{:S(2)}, u32[]{:S(2)}) collective-permute-start(bf16[1,784,128]{2,1,0:T(8,128)(2,1)S(1)} %collective-permute-done.7), channel_id=1, source_target_pairs={{0,56},{1,9},{8,0},{9,17},{16,8},{17,25},{24,16},{25,33},{32,24},{... | collective-permute-start | bytes 602120 | tf_op jit(solution)/shard_map/ppermute | solution.py:264
  55.6 13.3 %collective-permute-start.4 = (bf16[1,784,128]{2,1,0:T(8,128)(2,1)S(1)}, bf16[1,784,128]{2,1,0:T(8,128)(2,1)S(1)}, u32[]{:S(2)}, u32[]{:S(2)}) collective-permute-start(bf16[1,784,128]{2,1,0:T(8,128)(2,1)S(1)} %collective-permute-done.3.refs_3_), channel_id=1, source_target_pairs={{0,56},{1,9},{8,0},{9,17},{16,8},{17,25},{24,16},{25,33},{32,24},{... | collective-permute-start | bytes 602120 | tf_op jit(solution)/shard_map/ppermute | solution.py:264
  57.7 8.0 %collective-permute-start.9 = (bf16[1,784,128]{2,1,0:T(8,128)(2,1)S(1)}, bf16[1,784,128]{2,1,0:T(8,128)(2,1)S(1)}, u32[]{:S(2)}, u32[]{:S(2)}) collective-permute-start(bf16[1,784,128]{2,1,0:T(8,128)(2,1)S(1)} %collective-permute-done.8.refs_2_), channel_id=1, source_target_pairs={{0,56},{1,9},{8,0},{9,17},{16,8},{17,25},{24,16},{25,33},{32,24},{... | collective-permute-start | bytes 602120 | tf_op jit(solution)/shard_map/ppermute | solution.py:264
  65.7 9.2 %collective-permute-start.10 = (bf16[1,784,128]{2,1,0:T(8,128)(2,1)S(1)}, bf16[1,784,128]{2,1,0:T(8,128)(2,1)S(1)}, u32[]{:S(2)}, u32[]{:S(2)}) collective-permute-start(bf16[1,784,128]{2,1,0:T(8,128)(2,1)S(1)} %collective-permute-done.9.refs_2_), channel_id=1, source_target_pairs={{0,56},{1,9},{8,0},{9,17},{16,8},{17,25},{24,16},{25,33},{32,24},{... | collective-permute-start | bytes 602120 | tf_op jit(solution)/shard_map/ppermute | solution.py:264
  68.9 8.3 %collective-permute-start.5 = (bf16[1,784,128]{2,1,0:T(8,128)(2,1)S(1)}, bf16[1,784,128]{2,1,0:T(8,128)(2,1)S(1)}, u32[]{:S(2)}, u32[]{:S(2)}) collective-permute-start(bf16[1,784,128]{2,1,0:T(8,128)(2,1)S(1)} %collective-permute-done.4.refs_3_), channel_id=1, source_target_pairs={{0,56},{1,9},{8,0},{9,17},{16,8},{17,25},{24,16},{25,33},{32,24},{... | collective-permute-start | bytes 602120 | tf_op jit(solution)/shard_map/ppermute | solution.py:264
  78.0 10.1 %collective-permute-start.12 = (bf16[2,144,384]{2,1,0:T(8,128)(2,1)S(1)}, bf16[2,144,384]{2,1,0:T(8,128)(2,1)S(1)}, u32[]{:S(2)}, u32[]{:S(2)}) collective-permute-start(bf16[2,144,384]{2,1,0:T(8,128)(2,1)S(1)} %shard_map.57), channel_id=1, source_target_pairs={{0,1},{1,0},{2,3},{3,2},{4,5},{5,4},{6,7},{7,6},{8,9},{9,8},{10,11... | collective-permute-start | bytes 663560 | tf_op jit(solution)/shard_map/ppermute | solution.py:269
  85.3 6.9 %collective-permute-start.11 = (bf16[2,144,384]{2,1,0:T(8,128)(2,1)S(1)}, bf16[2,144,384]{2,1,0:T(8,128)(2,1)S(1)}, u32[]{:S(2)}, u32[]{:S(2)}) collective-permute-start(bf16[2,144,384]{2,1,0:T(8,128)(2,1)S(1)} %shard_map.55), channel_id=1, source_target_pairs={{0,1},{1,0},{2,3},{3,2},{4,5},{5,4},{6,7},{7,6},{8,9},{9,8},{10,11... | collective-permute-start | bytes 663560 | tf_op jit(solution)/shard_map/ppermute | solution.py:269
  88.2 8.4 %collective-permute-start.13 = (bf16[2,144,384]{2,1,0:T(8,128)(2,1)S(1)}, bf16[2,144,384]{2,1,0:T(8,128)(2,1)S(1)}, u32[]{:S(2)}, u32[]{:S(2)}) collective-permute-start(bf16[2,144,384]{2,1,0:T(8,128)(2,1)S(1)} %shard_map.58), channel_id=1, source_target_pairs={{0,64},{64,0},{1,65},{65,1},{2,66},{66,2},{3,67},{67,3},{4,68},{68... | collective-permute-start | bytes 663560 | tf_op jit(solution)/shard_map/ppermute | solution.py:269
